TPU v7x, 32 devices: a whole 2x2x4 slice. The times are simulated.
32 devices in a mesh: ccy: 4 (over x, core), path: 8 (over z, y).
Axes of the slice: x: 2, y: 2, z: 4, core: 2. Of those that a mesh axis runs over, the one named last changes fastest.
Arguments:
- curve_store: bfloat16 [4, 16, 64, 2048], P('ccy', 'path'), may hold values from -0.13 to 0.18
- cash_index: int32 [4, 2048, 16], P('ccy'), may hold values from 0 to 1023
- cash_amount: float32 [4, 2048, 16], P('ccy'), may hold values from -0.6 to 0.6
- trade_set: int32 [4, 2048], P('ccy'), may hold values from 0 to 511
- date_slot: int32 [16], replicated, may hold values from 0 to 15, as said below
- default_weight: float32 [16, 512], replicated, may hold values from 0.02 to 0.2
Outputs:
- exposure: float32 [16, 512], P(None, 'ccy')
- node_sens: float32 [4, 16, 64], P('ccy')
Inputs may be any that keep to these rules, and one draw needn't show every extreme that they name: `date_slot`: the 16 slots are distinct; slot s is stored at path index s // 2, position s % 2.
All inputs are finite; a program needn't handle non-finite values.
Results may differ from a plain program's by a relative error of at most 0.0029.
Values may be sent and summed in bfloat16 or wider, within the bound.
A program may use at most 64 MiB of HBM per device.

v0:
```python
import jax
import jax.numpy as jnp
from jax import lax
from jax.sharding import PartitionSpec as P

NODES = 64
CFG = 1024
NSETS = 512
DATES = 16
PATHS_DEV = 256


SOFTEN = 0.04
HORIZON = 32.0


def date_tables(date_index, node_count, grid_count):
    start_time = 0.5 * (jnp.asarray(date_index).astype(jnp.float32) + 1.0)
    grid_times = HORIZON * (jnp.arange(grid_count, dtype=jnp.float32) + 1.0) / grid_count
    tenors = HORIZON * (jnp.arange(node_count, dtype=jnp.float32) + 1.0) / node_count
    remain = grid_times - start_time
    alive_mask = (remain > 0.0).astype(jnp.float32)
    clipped = jnp.clip(remain, HORIZON / node_count, HORIZON)
    weights = jnp.maximum(
        0.0, 1.0 - jnp.abs(clipped[None, :] - tenors[:, None]) * (node_count / HORIZON)
    )
    return (remain, alive_mask, weights)


def netted_cash(flow_index, amount, trade_sets):
    columns = jnp.repeat(trade_sets, flow_index.shape[1])
    cash_table = (
        jnp.zeros((CFG, NSETS), jnp.float32)
        .at[flow_index.reshape(-1), columns]
        .add(amount.reshape(-1))
    )
    return cash_table.astype(jnp.bfloat16)


def local(curve_store, cash_index, cash_amount, trade_set, date_slot, default_weight):
    groups = lax.axis_size("ccy")
    group_index = lax.axis_index("ccy")
    share_size = NSETS // groups
    total_paths = PATHS_DEV * lax.axis_size("path")
    cash_table = netted_cash(cash_index[0], cash_amount[0], trade_set[0])
    blocks = lax.all_to_all(curve_store, "path", split_axis=3, concat_axis=1, tiled=True)[0]
    cash_all = lax.all_gather(cash_table[None], "ccy", axis=0, tiled=True)

    def fetch_curve(slot_id):
        found = lax.dynamic_index_in_dim(blocks, slot_id, 0, keepdims=False)
        return found

    def advance(unused, inputs):
        date_index, slot_id, weight_row = inputs
        remain, alive_mask, weights = date_tables(date_index, NODES, CFG)
        grid_weights = weights.astype(jnp.bfloat16)
        curve_now = fetch_curve(slot_id)
        curve_groups = lax.all_gather(curve_now[None], "ccy", axis=0, tiled=True)
        yields = jnp.einsum(
            "gnp,nc->gpc", curve_groups, grid_weights, preferred_element_type=jnp.float32
        )
        discount_all = alive_mask * jnp.exp(-yields * remain)
        values = jnp.einsum(
            "gpc,gcs->ps",
            discount_all.astype(jnp.bfloat16),
            cash_all,
            preferred_element_type=jnp.float32,
        )
        discount = lax.dynamic_index_in_dim(discount_all, group_index, 0, keepdims=False)
        rooted = jnp.sqrt(values * values + SOFTEN)
        slopes = (weight_row / total_paths * 0.5 * (1.0 + values / rooted)).astype(jnp.bfloat16)
        share_values = lax.dynamic_slice_in_dim(values, group_index * share_size, share_size, 1)
        share_root = lax.dynamic_slice_in_dim(rooted, group_index * share_size, share_size, 1)
        exposure_part = jnp.sum(0.5 * (share_values + share_root), axis=0) / total_paths
        back_flow = lax.dot_general(
            slopes, cash_table, (((1,), (1,)), ((), ())), preferred_element_type=jnp.float32
        )
        node_pull = jnp.sum(back_flow * -remain * discount, axis=0)
        sens_part = jnp.dot(weights, node_pull, precision=lax.Precision.HIGHEST)
        exposure_part, sens_part = lax.psum((exposure_part, sens_part), "path")
        return (unused, (exposure_part, sens_part))

    inputs = (jnp.arange(DATES, dtype=jnp.int32), date_slot, default_weight)
    unused, (exposure_rows, sens_rows) = lax.scan(advance, jnp.zeros((), jnp.float32), inputs)
    return (exposure_rows, sens_rows[None])


def solution(mesh):
    in_specs = (
        P("ccy", "path", None, None),
        P("ccy", None, None),
        P("ccy", None, None),
        P("ccy", None),
        P(),
        P(),
    )
    out_specs = (P(None, "ccy"), P("ccy", None, None))
    return jax.shard_map(local, mesh=mesh, in_specs=in_specs, out_specs=out_specs, check_vma=False)
```

profile of v0, /device:TPU:0, one launch (start us, length us, event | category | flops | bytes accessed | tf_op | source)
XLA Modules:
  0.0 758.6 jit_solution(14273269540718407822)
XLA Ops:
  12.4 171.6 %scatter_custom_fusion = f32[524288]{0:T(1024)S(1)} fusion(s32[32768]{0:T(1024)S(1)} %broadcast_select_fusion, f32[32768]{0:T(1024)S(1)} %reshape.107, f32[]{:T(128)} %constant.137.clone.1), kind=kCustom, calls=%fused_computation.43 | custom fusion | flops 32768 | bytes 2097156
  189.5 7.3 all-to-all-start
  197.5 13.8 %all-to-all-done = bf16[8,2,16384]{2,1,0:T(2,128)(2,1)S(1)} async-done(((bf16[8,2,16384]{2,1,0:T(2,128)(2,1)}), bf16[8,2,16384]{2,1,0:T(2,128)(2,1)S(1)}, u32[]{:S(2)}, u32[]{:S(2)}) %all-to-all-start) | async-done | bytes 524320 | tf_op jit(solution)/shard_map/all_to_all | solution.py:46
  212.6 10.3 %all-gather.2.cloned.1.call-done = bf16[4,1024,512]{2,1,0:T(8,128)(2,1)} async-done(((bf16[1,1024,512]{2,1,0:T(8,128)(2,1)}), bf16[4,1024,512]{2,1,0:T(8,128)(2,1)}) %all-gather.2.cloned.1.call-update) | async-done | bytes 4194320 | tf_op jit(solution)/shard_map/all_gather | solution.py:47
  222.9 528.2 %while.15 = (s32[]{:T(128)}, f32[16,128]{1,0:T(8,128)S(1)}, f32[16,64]{1,0:T(8,128)}, s32[16]{0:T(128)S(1)}, s32[16]{0:T(128)S(1)}, /*index=5*/bf16[16,64,256]{2...) while((s32[]{:T(128)}, f32[16,128]{1,0:T(8,128)S(1)}, ...), condition=%wide.region_6.7_spmd, body=%wide.region_1.6_spmd.sunk | while | flops 1484043008 | bytes 33709876 | solution.py:84
  236.3 21.4 %all-reduce.2 = (f32[1,128]{1,0:T(1,128)S(1)}, f32[1,64]{1,0:T(1,128)S(1)}) all-reduce(f32[1,128]{1,0:T(1,128)S(1)} %multiply_bitcast_fusion.2, f32[1,64]{1,0:T(1,128)S(1)} %fusion.54), channel_id=1, replica_groups=mesh['ccy'=4,'path'=8] {'path'}, use_global_device_ids=true, to_apply=%region_3.3 | all-reduce | flops 192 | bytes 1536 | tf_op jit(solution)/shard_map/while/body/eval_jaxpr/psum | solution.py:80
  272.4 17.2 %all-reduce.2 = (f32[1,128]{1,0:T(1,128)S(1)}, f32[1,64]{1,0:T(1,128)S(1)}) all-reduce(f32[1,128]{1,0:T(1,128)S(1)} %multiply_bitcast_fusion.2, f32[1,64]{1,0:T(1,128)S(1)} %fusion.54), channel_id=1, replica_groups=mesh['ccy'=4,'path'=8] {'path'}, use_global_device_ids=true, to_apply=%region_3.3 | all-reduce | flops 192 | bytes 1536 | tf_op jit(solution)/shard_map/while/body/eval_jaxpr/psum | solution.py:80
  304.3 19.2 %all-reduce.2 = (f32[1,128]{1,0:T(1,128)S(1)}, f32[1,64]{1,0:T(1,128)S(1)}) all-reduce(f32[1,128]{1,0:T(1,128)S(1)} %multiply_bitcast_fusion.2, f32[1,64]{1,0:T(1,128)S(1)} %fusion.54), channel_id=1, replica_groups=mesh['ccy'=4,'path'=8] {'path'}, use_global_device_ids=true, to_apply=%region_3.3 | all-reduce | flops 192 | bytes 1536 | tf_op jit(solution)/shard_map/while/body/eval_jaxpr/psum | solution.py:80
  338.2 17.2 %all-reduce.2 = (f32[1,128]{1,0:T(1,128)S(1)}, f32[1,64]{1,0:T(1,128)S(1)}) all-reduce(f32[1,128]{1,0:T(1,128)S(1)} %multiply_bitcast_fusion.2, f32[1,64]{1,0:T(1,128)S(1)} %fusion.54), channel_id=1, replica_groups=mesh['ccy'=4,'path'=8] {'path'}, use_global_device_ids=true, to_apply=%region_3.3 | all-reduce | flops 192 | bytes 1536 | tf_op jit(solution)/shard_map/while/body/eval_jaxpr/psum | solution.py:80
  370.1 19.2 %all-reduce.2 = (f32[1,128]{1,0:T(1,128)S(1)}, f32[1,64]{1,0:T(1,128)S(1)}) all-reduce(f32[1,128]{1,0:T(1,128)S(1)} %multiply_bitcast_fusion.2, f32[1,64]{1,0:T(1,128)S(1)} %fusion.54), channel_id=1, replica_groups=mesh['ccy'=4,'path'=8] {'path'}, use_global_device_ids=true, to_apply=%region_3.3 | all-reduce | flops 192 | bytes 1536 | tf_op jit(solution)/shard_map/while/body/eval_jaxpr/psum | solution.py:80
  403.9 17.2 %all-reduce.2 = (f32[1,128]{1,0:T(1,128)S(1)}, f32[1,64]{1,0:T(1,128)S(1)}) all-reduce(f32[1,128]{1,0:T(1,128)S(1)} %multiply_bitcast_fusion.2, f32[1,64]{1,0:T(1,128)S(1)} %fusion.54), channel_id=1, replica_groups=mesh['ccy'=4,'path'=8] {'path'}, use_global_device_ids=true, to_apply=%region_3.3 | all-reduce | flops 192 | bytes 1536 | tf_op jit(solution)/shard_map/while/body/eval_jaxpr/psum | solution.py:80
  435.8 19.2 %all-reduce.2 = (f32[1,128]{1,0:T(1,128)S(1)}, f32[1,64]{1,0:T(1,128)S(1)}) all-reduce(f32[1,128]{1,0:T(1,128)S(1)} %multiply_bitcast_fusion.2, f32[1,64]{1,0:T(1,128)S(1)} %fusion.54), channel_id=1, replica_groups=mesh['ccy'=4,'path'=8] {'path'}, use_global_device_ids=true, to_apply=%region_3.3 | all-reduce | flops 192 | bytes 1536 | tf_op jit(solution)/shard_map/while/body/eval_jaxpr/psum | solution.py:80
  469.7 17.2 %all-reduce.2 = (f32[1,128]{1,0:T(1,128)S(1)}, f32[1,64]{1,0:T(1,128)S(1)}) all-reduce(f32[1,128]{1,0:T(1,128)S(1)} %multiply_bitcast_fusion.2, f32[1,64]{1,0:T(1,128)S(1)} %fusion.54), channel_id=1, replica_groups=mesh['ccy'=4,'path'=8] {'path'}, use_global_device_ids=true, to_apply=%region_3.3 | all-reduce | flops 192 | bytes 1536 | tf_op jit(solution)/shard_map/while/body/eval_jaxpr/psum | solution.py:80
  501.6 19.2 %all-reduce.2 = (f32[1,128]{1,0:T(1,128)S(1)}, f32[1,64]{1,0:T(1,128)S(1)}) all-reduce(f32[1,128]{1,0:T(1,128)S(1)} %multiply_bitcast_fusion.2, f32[1,64]{1,0:T(1,128)S(1)} %fusion.54), channel_id=1, replica_groups=mesh['ccy'=4,'path'=8] {'path'}, use_global_device_ids=true, to_apply=%region_3.3 | all-reduce | flops 192 | bytes 1536 | tf_op jit(solution)/shard_map/while/body/eval_jaxpr/psum | solution.py:80
  524.5 5.5 all_gather.12
  535.4 17.2 %all-reduce.2 = (f32[1,128]{1,0:T(1,128)S(1)}, f32[1,64]{1,0:T(1,128)S(1)}) all-reduce(f32[1,128]{1,0:T(1,128)S(1)} %multiply_bitcast_fusion.2, f32[1,64]{1,0:T(1,128)S(1)} %fusion.54), channel_id=1, replica_groups=mesh['ccy'=4,'path'=8] {'path'}, use_global_device_ids=true, to_apply=%region_3.3 | all-reduce | flops 192 | bytes 1536 | tf_op jit(solution)/shard_map/while/body/eval_jaxpr/psum | solution.py:80
  567.3 19.2 %all-reduce.2 = (f32[1,128]{1,0:T(1,128)S(1)}, f32[1,64]{1,0:T(1,128)S(1)}) all-reduce(f32[1,128]{1,0:T(1,128)S(1)} %multiply_bitcast_fusion.2, f32[1,64]{1,0:T(1,128)S(1)} %fusion.54), channel_id=1, replica_groups=mesh['ccy'=4,'path'=8] {'path'}, use_global_device_ids=true, to_apply=%region_3.3 | all-reduce | flops 192 | bytes 1536 | tf_op jit(solution)/shard_map/while/body/eval_jaxpr/psum | solution.py:80
  590.3 5.5 all_gather.12
  601.2 17.2 %all-reduce.2 = (f32[1,128]{1,0:T(1,128)S(1)}, f32[1,64]{1,0:T(1,128)S(1)}) all-reduce(f32[1,128]{1,0:T(1,128)S(1)} %multiply_bitcast_fusion.2, f32[1,64]{1,0:T(1,128)S(1)} %fusion.54), channel_id=1, replica_groups=mesh['ccy'=4,'path'=8] {'path'}, use_global_device_ids=true, to_apply=%region_3.3 | all-reduce | flops 192 | bytes 1536 | tf_op jit(solution)/shard_map/while/body/eval_jaxpr/psum | solution.py:80
  633.1 19.2 %all-reduce.2 = (f32[1,128]{1,0:T(1,128)S(1)}, f32[1,64]{1,0:T(1,128)S(1)}) all-reduce(f32[1,128]{1,0:T(1,128)S(1)} %multiply_bitcast_fusion.2, f32[1,64]{1,0:T(1,128)S(1)} %fusion.54), channel_id=1, replica_groups=mesh['ccy'=4,'path'=8] {'path'}, use_global_device_ids=true, to_apply=%region_3.3 | all-reduce | flops 192 | bytes 1536 | tf_op jit(solution)/shard_map/while/body/eval_jaxpr/psum | solution.py:80
  656.0 5.5 all_gather.12
  666.9 17.2 %all-reduce.2 = (f32[1,128]{1,0:T(1,128)S(1)}, f32[1,64]{1,0:T(1,128)S(1)}) all-reduce(f32[1,128]{1,0:T(1,128)S(1)} %multiply_bitcast_fusion.2, f32[1,64]{1,0:T(1,128)S(1)} %fusion.54), channel_id=1, replica_groups=mesh['ccy'=4,'path'=8] {'path'}, use_global_device_ids=true, to_apply=%region_3.3 | all-reduce | flops 192 | bytes 1536 | tf_op jit(solution)/shard_map/while/body/eval_jaxpr/psum | solution.py:80
  698.8 19.2 %all-reduce.2 = (f32[1,128]{1,0:T(1,128)S(1)}, f32[1,64]{1,0:T(1,128)S(1)}) all-reduce(f32[1,128]{1,0:T(1,128)S(1)} %multiply_bitcast_fusion.2, f32[1,64]{1,0:T(1,128)S(1)} %fusion.54), channel_id=1, replica_groups=mesh['ccy'=4,'path'=8] {'path'}, use_global_device_ids=true, to_apply=%region_3.3 | all-reduce | flops 192 | bytes 1536 | tf_op jit(solution)/shard_map/while/body/eval_jaxpr/psum | solution.py:80
  732.7 17.2 %all-reduce.2 = (f32[1,128]{1,0:T(1,128)S(1)}, f32[1,64]{1,0:T(1,128)S(1)}) all-reduce(f32[1,128]{1,0:T(1,128)S(1)} %multiply_bitcast_fusion.2, f32[1,64]{1,0:T(1,128)S(1)} %fusion.54), channel_id=1, replica_groups=mesh['ccy'=4,'path'=8] {'path'}, use_global_device_ids=true, to_apply=%region_3.3 | all-reduce | flops 192 | bytes 1536 | tf_op jit(solution)/shard_map/while/body/eval_jaxpr/psum | solution.py:80
  (333 shorter events, 191.0 us)
Async XLA Ops:
  7.2 3.5 copy-start.2
  7.2 4.1 copy-start.3
  7.2 4.6 copy-start.1
  7.2 215.7 %all-gather.2.cloned.1.call-start = ((), (), s32[]{:S(2)}) async-start(), calls=%async_computation.1 | async-start | bytes 5242880 | tf_op jit(solution)/shard_map/all_gather | solution.py:47
  188.0 35.0 %copy-start.5 = (s32[16]{0:T(128)S(1)}, s32[16]{0:T(128)}, u32[]{:S(2)}) copy-start(s32[16]{0:T(128)} %param.12) | copy-start | bytes 196
  189.5 21.8 %all-to-all-start = ((bf16[8,2,16384]{2,1,0:T(2,128)(2,1)}), bf16[8,2,16384]{2,1,0:T(2,128)(2,1)S(1)}, u32[]{:S(2)}, u32[]{:S(2)}) async-start(bf16[8,2,16384]{2,1,0:T(2,128)(2,1)} %reshape.117), calls=%async_computation | async-start | bytes 1048576 | tf_op jit(solution)/shard_map/all_to_all | solution.py:46
  225.4 7.8 %copy-start = (bf16[4,1024,512]{2,1,0:T(8,128)(2,1)S(1)}, bf16[4,1024,512]{2,1,0:T(8,128)(2,1)}, u32[]{:S(2)}) copy-start(bf16[4,1024,512]{2,1,0:T(8,128)(2,1)} %get-tuple-element.337) | copy-start | bytes 12582916 | tf_op jit(solution)/shard_map/while
  261.5 7.8 %copy-start = (bf16[4,1024,512]{2,1,0:T(8,128)(2,1)S(1)}, bf16[4,1024,512]{2,1,0:T(8,128)(2,1)}, u32[]{:S(2)}) copy-start(bf16[4,1024,512]{2,1,0:T(8,128)(2,1)} %get-tuple-element.337) | copy-start | bytes 12582916 | tf_op jit(solution)/shard_map/while
  293.4 7.8 %copy-start = (bf16[4,1024,512]{2,1,0:T(8,128)(2,1)S(1)}, bf16[4,1024,512]{2,1,0:T(8,128)(2,1)}, u32[]{:S(2)}) copy-start(bf16[4,1024,512]{2,1,0:T(8,128)(2,1)} %get-tuple-element.337) | copy-start | bytes 12582916 | tf_op jit(solution)/shard_map/while
  327.2 7.8 %copy-start = (bf16[4,1024,512]{2,1,0:T(8,128)(2,1)S(1)}, bf16[4,1024,512]{2,1,0:T(8,128)(2,1)}, u32[]{:S(2)}) copy-start(bf16[4,1024,512]{2,1,0:T(8,128)(2,1)} %get-tuple-element.337) | copy-start | bytes 12582916 | tf_op jit(solution)/shard_map/while
  359.1 7.8 %copy-start = (bf16[4,1024,512]{2,1,0:T(8,128)(2,1)S(1)}, bf16[4,1024,512]{2,1,0:T(8,128)(2,1)}, u32[]{:S(2)}) copy-start(bf16[4,1024,512]{2,1,0:T(8,128)(2,1)} %get-tuple-element.337) | copy-start | bytes 12582916 | tf_op jit(solution)/shard_map/while
  393.0 7.8 %copy-start = (bf16[4,1024,512]{2,1,0:T(8,128)(2,1)S(1)}, bf16[4,1024,512]{2,1,0:T(8,128)(2,1)}, u32[]{:S(2)}) copy-start(bf16[4,1024,512]{2,1,0:T(8,128)(2,1)} %get-tuple-element.337) | copy-start | bytes 12582916 | tf_op jit(solution)/shard_map/while
  424.9 7.8 %copy-start = (bf16[4,1024,512]{2,1,0:T(8,128)(2,1)S(1)}, bf16[4,1024,512]{2,1,0:T(8,128)(2,1)}, u32[]{:S(2)}) copy-start(bf16[4,1024,512]{2,1,0:T(8,128)(2,1)} %get-tuple-element.337) | copy-start | bytes 12582916 | tf_op jit(solution)/shard_map/while
  458.7 7.8 %copy-start = (bf16[4,1024,512]{2,1,0:T(8,128)(2,1)S(1)}, bf16[4,1024,512]{2,1,0:T(8,128)(2,1)}, u32[]{:S(2)}) copy-start(bf16[4,1024,512]{2,1,0:T(8,128)(2,1)} %get-tuple-element.337) | copy-start | bytes 12582916 | tf_op jit(solution)/shard_map/while
  490.6 7.8 %copy-start = (bf16[4,1024,512]{2,1,0:T(8,128)(2,1)S(1)}, bf16[4,1024,512]{2,1,0:T(8,128)(2,1)}, u32[]{:S(2)}) copy-start(bf16[4,1024,512]{2,1,0:T(8,128)(2,1)} %get-tuple-element.337) | copy-start | bytes 12582916 | tf_op jit(solution)/shard_map/while
  524.5 7.8 %copy-start = (bf16[4,1024,512]{2,1,0:T(8,128)(2,1)S(1)}, bf16[4,1024,512]{2,1,0:T(8,128)(2,1)}, u32[]{:S(2)}) copy-start(bf16[4,1024,512]{2,1,0:T(8,128)(2,1)} %get-tuple-element.337) | copy-start | bytes 12582916 | tf_op jit(solution)/shard_map/while
  556.4 7.8 %copy-start = (bf16[4,1024,512]{2,1,0:T(8,128)(2,1)S(1)}, bf16[4,1024,512]{2,1,0:T(8,128)(2,1)}, u32[]{:S(2)}) copy-start(bf16[4,1024,512]{2,1,0:T(8,128)(2,1)} %get-tuple-element.337) | copy-start | bytes 12582916 | tf_op jit(solution)/shard_map/while
  590.3 7.8 %copy-start = (bf16[4,1024,512]{2,1,0:T(8,128)(2,1)S(1)}, bf16[4,1024,512]{2,1,0:T(8,128)(2,1)}, u32[]{:S(2)}) copy-start(bf16[4,1024,512]{2,1,0:T(8,128)(2,1)} %get-tuple-element.337) | copy-start | bytes 12582916 | tf_op jit(solution)/shard_map/while
  622.1 7.8 %copy-start = (bf16[4,1024,512]{2,1,0:T(8,128)(2,1)S(1)}, bf16[4,1024,512]{2,1,0:T(8,128)(2,1)}, u32[]{:S(2)}) copy-start(bf16[4,1024,512]{2,1,0:T(8,128)(2,1)} %get-tuple-element.337) | copy-start | bytes 12582916 | tf_op jit(solution)/shard_map/while
  656.0 7.8 %copy-start = (bf16[4,1024,512]{2,1,0:T(8,128)(2,1)S(1)}, bf16[4,1024,512]{2,1,0:T(8,128)(2,1)}, u32[]{:S(2)}) copy-start(bf16[4,1024,512]{2,1,0:T(8,128)(2,1)} %get-tuple-element.337) | copy-start | bytes 12582916 | tf_op jit(solution)/shard_map/while
  687.9 7.8 %copy-start = (bf16[4,1024,512]{2,1,0:T(8,128)(2,1)S(1)}, bf16[4,1024,512]{2,1,0:T(8,128)(2,1)}, u32[]{:S(2)}) copy-start(bf16[4,1024,512]{2,1,0:T(8,128)(2,1)} %get-tuple-element.337) | copy-start | bytes 12582916 | tf_op jit(solution)/shard_map/while
  721.8 7.8 %copy-start = (bf16[4,1024,512]{2,1,0:T(8,128)(2,1)S(1)}, bf16[4,1024,512]{2,1,0:T(8,128)(2,1)}, u32[]{:S(2)}) copy-start(bf16[4,1024,512]{2,1,0:T(8,128)(2,1)} %get-tuple-element.337) | copy-start | bytes 12582916 | tf_op jit(solution)/shard_map/while
  751.2 0.6 copy-start.4
Sparse Core Ops, SparseCore 0:
  185.7 37.1 all-gather.1
where the time goes:
time: 762 us; the launch traced here: 759 us
  blocking collectives  382 us (50%)
  other arithmetic  187 us (25%)
  matrix products  52 us (7%)
  local copies, waits for them, and re-layouts  51.8 us (7%)
  loops' own time  40.8 us (5%)
  waiting for transfers between devices  24.2 us (3%)
  between operations  14.2 us (2%)
    psum x16, blocking collectives, advance(): exposure_part, sens_part = lax.psum((exposure_part, sens_part), 'path')  293 us
    unnamed x4, other arithmetic  173 us
    all_gather x16, blocking collectives, advance(): curve_groups = lax.all_gather(curve_now[None], 'ccy', axis=0, tiled=True)  88.8 us
    another operation x1, loops' own time, local(): lax.scan(advance, jnp.zeros((), jnp.float32), inputs)  40.8 us
    dot_general x16, matrix products, advance(): jnp.einsum('gpc,gcs->ps', discount_all.astype(jnp.bfloat16), cash_all, pr...  21.4 us
    dynamic_update_slice x32, local copies, waits for them, and re-layouts, local(): lax.scan(advance, jnp.zeros((), jnp.float32), inputs)  21.1 us
    dynamic_slice x32, local copies, waits for them, and re-layouts, local(): lax.scan(advance, jnp.zeros((), jnp.float32), inputs)  18.9 us
  transfers between devices with their start and end apart: 2, of which 2 were waited for; matrix products, arithmetic and copies ran while one was open for 1% of the time, Pallas kernels for 0%

commit v1 on v0

--- a/solution.py
+++ b/solution.py
@@ -1,17 +1,18 @@
+import functools
+
 import jax
 import jax.numpy as jnp
 from jax import lax
+from jax.experimental import pallas as pl
+from jax.experimental.pallas import tpu as pltpu
 from jax.sharding import PartitionSpec as P
 
-NODES = 64
+NSETS = 512
 CFG = 1024
-NSETS = 512
-DATES = 16
-PATHS_DEV = 256
-
-
 SOFTEN = 0.04
 HORIZON = 32.0
+LOG2E = 1.4426950408889634
+COLS = 256
 
 
 def date_tables(date_index, node_count, grid_count):
@@ -27,43 +28,189 @@
     return (remain, alive_mask, weights)
 
 
-def netted_cash(flow_index, amount, trade_sets):
-    columns = jnp.repeat(trade_sets, flow_index.shape[1])
-    cash_table = (
-        jnp.zeros((CFG, NSETS), jnp.float32)
-        .at[flow_index.reshape(-1), columns]
-        .add(amount.reshape(-1))
-    )
-    return cash_table.astype(jnp.bfloat16)
-
-
-def local(curve_store, cash_index, cash_amount, trade_set, date_slot, default_weight):
+def cash_kernel(rows, base_ref, index_ref, amount_ref, set_ref, out_ref, a_hi, a_lo):
+    flows, trades = index_ref.shape
+    nsets = out_ref.shape[1]
+    wanted = lax.broadcasted_iota(jnp.int32, (rows, 128), 0) + base_ref[0]
+
+    @pl.loop(0, trades // 128)
+    def _(tile):
+        cols = pl.ds(pl.multiple_of(tile * 128, 128), 128)
+        total = jnp.zeros((rows, 128), jnp.float32)
+        index = index_ref[:, cols]
+        amount = amount_ref[:, cols]
+        for k in range(flows):
+            hit = wanted == index[k : k + 1, :]
+            total = total + jnp.where(hit, amount[k : k + 1, :], 0.0)
+        high = total.astype(jnp.bfloat16)
+        a_hi[:, cols] = high
+        a_lo[:, cols] = (total - high.astype(jnp.float32)).astype(jnp.bfloat16)
+
+    sets = lax.broadcasted_iota(jnp.int32, (nsets, trades), 0)
+    onehot = jnp.where(sets == set_ref[...], 1.0, 0.0).astype(jnp.bfloat16)
+    dims = (((1,), (1,)), ((), ()))
+    table = lax.dot_general(a_hi[...], onehot, dims, preferred_element_type=jnp.float32)
+    table = table + lax.dot_general(a_lo[...], onehot, dims, preferred_element_type=jnp.float32)
+    out_ref[...] = table.astype(jnp.bfloat16)
+
+
+def build_cash(base, flow_index, amount, trade_sets, rows, nsets):
+    flows, trades = flow_index.shape[1], flow_index.shape[0]
+    vmem = pl.BlockSpec(memory_space=pltpu.VMEM)
+    return pl.pallas_call(
+        functools.partial(cash_kernel, rows),
+        out_shape=jax.ShapeDtypeStruct((rows, nsets), jnp.bfloat16),
+        in_specs=[pl.BlockSpec(memory_space=pltpu.SMEM), vmem, vmem, vmem],
+        out_specs=vmem,
+        scratch_shapes=[pltpu.VMEM((rows, trades), jnp.bfloat16)] * 2,
+        cost_estimate=pl.CostEstimate(
+            flops=4 * rows * trades * nsets, bytes_accessed=4 * trades * flows, transcendentals=0
+        ),
+        name="cash_rows",
+    )(base, flow_index.T, amount.T, trade_sets[None, :])
+
+
+def main_kernel(groups, cfg, total_paths, date_ref, curve_ref, cash_ref, dw_ref, exp_ref, sens_ref, disc):
+    nodes, paths = curve_ref.shape[2], curve_ref.shape[3]
+    date = date_ref[pl.program_id(0)]
+    start_time = 0.5 * (date.astype(jnp.float32) + 1.0)
+    step = HORIZON / cfg
+    tenors = (lax.broadcasted_iota(jnp.int32, (nodes, COLS), 0).astype(jnp.float32) + 1.0) * (HORIZON / nodes)
+    per_group = cfg // COLS
+
+    def tables(block):
+        at = lax.broadcasted_iota(jnp.int32, (1, COLS), 1) + block * COLS
+        remain = (at.astype(jnp.float32) + 1.0) * step - start_time
+        clipped = jnp.clip(remain, HORIZON / nodes, HORIZON)
+        weights = jnp.maximum(0.0, 1.0 - jnp.abs(clipped - tenors) * (nodes / HORIZON))
+        return remain, weights
+
+    for block in range(per_group):
+        remain, weights = tables(block)
+        weights = weights.astype(jnp.bfloat16)
+        scaled = remain * (-LOG2E)
+        alive = remain > 0.0
+        for g in range(groups):
+            rate = lax.dot_general(
+                curve_ref[g, 0], weights, (((0,), (0,)), ((), ())), preferred_element_type=jnp.float32
+            )
+            value = jnp.where(alive, jnp.exp2(rate * scaled), 0.0)
+            disc[:, pl.ds(g * cfg + block * COLS, COLS)] = value.astype(jnp.bfloat16)
+
+    values = jnp.dot(disc[...], cash_ref[...], preferred_element_type=jnp.float32)
+    square = values * values + SOFTEN
+    inverse = lax.rsqrt(square)
+    exp_ref[0] = jnp.sum(0.5 * (values + square * inverse), axis=0, keepdims=True) / total_paths
+    row = dw_ref[pl.ds(date, 1), :] / total_paths * 0.5
+    slopes = (row * (1.0 + values * inverse)).astype(jnp.bfloat16)
+
+    for g in range(groups):
+        sens = jnp.zeros((8, nodes), jnp.float32)
+        for block in range(per_group):
+            at = g * cfg + block * COLS
+            back = lax.dot_general(
+                slopes, cash_ref[pl.ds(at, COLS), :], (((1,), (1,)), ((), ())),
+                preferred_element_type=jnp.float32,
+            )
+            summed = jnp.sum(back * disc[:, pl.ds(at, COLS)].astype(jnp.float32), axis=0, keepdims=True)
+            remain, weights = tables(block)
+            pull = jnp.broadcast_to(summed * -remain, (8, COLS))
+            weights = weights.astype(jnp.bfloat16)
+            for _ in range(3):
+                piece = pull.astype(jnp.bfloat16)
+                pull = pull - piece.astype(jnp.float32)
+                sens = sens + lax.dot_general(
+                    piece, weights, (((1,), (1,)), ((), ())), preferred_element_type=jnp.float32
+                )
+        sens_ref[0, g : g + 1, :] = sens[0:1, :]
+
+
+def run_main(dates, curves, cash, default_weight, total_paths):
+    groups, slots, nodes, paths = curves.shape
+    rows, nsets = cash.shape
+    cfg = rows // groups
+    work = slots * paths * rows * (4 * nsets + 2 * nodes)
+    return pl.pallas_call(
+        functools.partial(main_kernel, groups, cfg, total_paths),
+        grid=(slots,),
+        out_shape=[
+            jax.ShapeDtypeStruct((slots, 1, nsets), jnp.float32),
+            jax.ShapeDtypeStruct((slots, groups, nodes), jnp.float32),
+        ],
+        in_specs=[
+            pl.BlockSpec(memory_space=pltpu.SMEM),
+            pl.BlockSpec((groups, 1, nodes, paths), lambda s: (0, s, 0, 0)),
+            pl.BlockSpec(memory_space=pltpu.VMEM),
+            pl.BlockSpec(memory_space=pltpu.VMEM),
+        ],
+        out_specs=[
+            pl.BlockSpec((1, 1, nsets), lambda s: (s, 0, 0)),
+            pl.BlockSpec((1, groups, nodes), lambda s: (s, 0, 0)),
+        ],
+        scratch_shapes=[pltpu.VMEM((paths, rows), jnp.bfloat16)],
+        cost_estimate=pl.CostEstimate(
+            flops=work, bytes_accessed=rows * nsets * 2, transcendentals=slots * paths * rows
+        ),
+        name="price_dates",
+    )(dates, curves, cash, default_weight)
+
+
+def by_slot(curve_store, cash_index, cash_amount, trade_set, date_slot, default_weight):
+    groups, members = lax.axis_size("ccy"), lax.axis_size("path")
+    group_index, path_index = lax.axis_index("ccy"), lax.axis_index("path")
+    slots = curve_store.shape[1]
+    nodes = curve_store.shape[2]
+    total_paths = curve_store.shape[3]
+    rows = CFG // members
+    nsets = default_weight.shape[1]
+    base = (path_index * rows).astype(jnp.int32)[None]
+    curves = lax.all_to_all(curve_store, "ccy", split_axis=3, concat_axis=0, tiled=True)
+    chunk = build_cash(base, cash_index[0], cash_amount[0], trade_set[0], rows, nsets)
+    cash = lax.all_gather(chunk, ("ccy", "path"), axis=0, tiled=True)
+    own = path_index * slots + jnp.arange(slots, dtype=jnp.int32)
+    numbers = jnp.arange(date_slot.shape[0], dtype=jnp.int32)
+    dates = jnp.sum(jnp.where(date_slot[None, :] == own[:, None], numbers[None, :], 0), axis=1).astype(jnp.int32)
+    exposure_part, sens_part = run_main(dates, curves, cash, default_weight, total_paths)
+    part = jnp.concatenate([exposure_part[:, 0, :], sens_part.reshape(slots, groups * nodes)], axis=1)
+    parts = lax.all_gather(part, ("ccy", "path"), axis=0)
+    share = nsets // groups
+    exposure = lax.dynamic_slice_in_dim(parts, group_index * share, share, 2)
+    sens = lax.dynamic_slice_in_dim(parts, nsets + group_index * nodes, nodes, 2)
+
+    def finish(block):
+        rows_by_slot = jnp.sum(block.reshape(groups, members * slots, -1), axis=0)
+        hit = date_slot[:, None, None] == jnp.arange(members * slots, dtype=jnp.int32)[None, :, None]
+        return jnp.sum(jnp.where(hit, rows_by_slot[None], 0.0), axis=1)
+
+    return (finish(exposure), finish(sens)[None])
+
+
+def by_path(curve_store, cash_index, cash_amount, trade_set, date_slot, default_weight):
     groups = lax.axis_size("ccy")
     group_index = lax.axis_index("ccy")
-    share_size = NSETS // groups
-    total_paths = PATHS_DEV * lax.axis_size("path")
-    cash_table = netted_cash(cash_index[0], cash_amount[0], trade_set[0])
+    members = lax.axis_size("path")
+    nodes, total_paths = curve_store.shape[2], curve_store.shape[3]
+    nsets = default_weight.shape[1]
+    share_size = nsets // groups
+    rows = CFG // members
+    base = (lax.axis_index("path") * rows).astype(jnp.int32)[None]
+    chunk = build_cash(base, cash_index[0], cash_amount[0], trade_set[0], rows, nsets)
+    cash_table = lax.all_gather(chunk, "path", axis=0, tiled=True)
     blocks = lax.all_to_all(curve_store, "path", split_axis=3, concat_axis=1, tiled=True)[0]
     cash_all = lax.all_gather(cash_table[None], "ccy", axis=0, tiled=True)
 
-    def fetch_curve(slot_id):
-        found = lax.dynamic_index_in_dim(blocks, slot_id, 0, keepdims=False)
-        return found
-
     def advance(unused, inputs):
         date_index, slot_id, weight_row = inputs
-        remain, alive_mask, weights = date_tables(date_index, NODES, CFG)
+        remain, alive_mask, weights = date_tables(date_index, nodes, CFG)
         grid_weights = weights.astype(jnp.bfloat16)
-        curve_now = fetch_curve(slot_id)
+        curve_now = lax.dynamic_index_in_dim(blocks, slot_id, 0, keepdims=False)
         curve_groups = lax.all_gather(curve_now[None], "ccy", axis=0, tiled=True)
         yields = jnp.einsum(
             "gnp,nc->gpc", curve_groups, grid_weights, preferred_element_type=jnp.float32
         )
         discount_all = alive_mask * jnp.exp(-yields * remain)
         values = jnp.einsum(
-            "gpc,gcs->ps",
-            discount_all.astype(jnp.bfloat16),
-            cash_all,
+            "gpc,gcs->ps", discount_all.astype(jnp.bfloat16), cash_all,
             preferred_element_type=jnp.float32,
         )
         discount = lax.dynamic_index_in_dim(discount_all, group_index, 0, keepdims=False)
@@ -80,9 +227,15 @@
         exposure_part, sens_part = lax.psum((exposure_part, sens_part), "path")
         return (unused, (exposure_part, sens_part))
 
-    inputs = (jnp.arange(DATES, dtype=jnp.int32), date_slot, default_weight)
-    unused, (exposure_rows, sens_rows) = lax.scan(advance, jnp.zeros((), jnp.float32), inputs)
+    inputs = (jnp.arange(date_slot.shape[0], dtype=jnp.int32), date_slot, default_weight)
+    _, (exposure_rows, sens_rows) = lax.scan(advance, jnp.zeros((), jnp.float32), inputs)
     return (exposure_rows, sens_rows[None])
+
+
+def local(curve_store, cash_index, cash_amount, trade_set, date_slot, default_weight):
+    stored = curve_store.shape[1] * lax.axis_size("path")
+    plan = by_slot if stored == date_slot.shape[0] else by_path
+    return plan(curve_store, cash_index, cash_amount, trade_set, date_slot, default_weight)
 
 
 def solution(mesh):

time: 762 us -> 175 us (0.23)
  blocking collectives: 382 us -> 67.2 us
  other arithmetic: 187 us -> 2.29 us
  matrix products: 52 us -> 0 us
  local copies, waits for them, and re-layouts: 51.8 us -> 8.02 us
  loops' own time: 40.8 us -> 0 us
  waiting for transfers between devices: 24.2 us -> 53.6 us
  Pallas kernels: 0 us -> 25.2 us
    psum x16 -> x0, blocking collectives: 293 us -> none  [advance(): exposure_part, sens_part = lax.psum((exposure_part, sens_part), 'path')]
    unnamed x4 -> x1, other arithmetic: 173 us -> 0.01 us
    dot_general x64 -> x0, matrix products: 52 us -> none  [the longest x16 21.4 us: advance(): jnp.einsum('gpc,gcs->ps', discount_all.astype(jnp.bfloat16), cash_all, pr...]
    another operation x1 -> x0, loops' own time: 40.8 us -> none  [local(): lax.scan(advance, jnp.zeros((), jnp.float32), inputs)]
    all_gather x1, waiting for transfers between devices: 10.3 us -> 44.6 us  [by_slot(): cash = lax.all_gather(chunk, ('ccy', 'path'), axis=0, tiled=True)]
    pallas_call x0 -> x2, Pallas kernels: none -> 25.2 us  [the longest x1 20.2 us: run_main(): pl.pallas_call(functools.partial(main_kernel, groups, cfg, total_paths),...]
    all_gather x16 -> x1, blocking collectives: 88.8 us -> 67.2 us  [by_slot(): parts = lax.all_gather(part, ('ccy', 'path'), axis=0)]
    dynamic_update_slice x32 -> x0, local copies, waits for them, and re-layouts: 21.1 us -> none  [local(): lax.scan(advance, jnp.zeros((), jnp.float32), inputs)]
  transfers between devices with their start and end apart: 2 -> 2, of which waited for: 2 -> 2; matrix products, arithmetic and copies ran while one was open for 1% -> 4% of each run, Pallas kernels for 0% -> 0%
where the time goes in v1:
time: 175 us
  blocking collectives  67.2 us (38%)
  waiting for transfers between devices  53.6 us (31%)
  Pallas kernels  25.2 us (14%)
  between operations  14.1 us (8%)
  local copies, waits for them, and re-layouts  8.02 us (5%)
  starting transfers between devices  4.27 us (2%)
  other arithmetic  2.29 us (1%)
    all_gather x1, blocking collectives, by_slot(): parts = lax.all_gather(part, ('ccy', 'path'), axis=0)  67.2 us
    all_gather x1, waiting for transfers between devices, by_slot(): cash = lax.all_gather(chunk, ('ccy', 'path'), axis=0, tiled=True)  44.6 us
    pallas_call x1, Pallas kernels, run_main(): pl.pallas_call(functools.partial(main_kernel, groups, cfg, total_paths),...  20.2 us
    all_to_all x1, waiting for transfers between devices, by_slot(): lax.all_to_all(curve_store, 'ccy', split_axis=3, concat_axis=0, tiled=True)  8.91 us
    unnamed x6, local copies, waits for them, and re-layouts  5.31 us
    pallas_call x1, Pallas kernels, build_cash(): pl.pallas_call(functools.partial(cash_kernel, rows), out_shape=jax.ShapeD...  5.05 us
    all_to_all x1, starting transfers between devices, by_slot(): lax.all_to_all(curve_store, 'ccy', split_axis=3, concat_axis=0, tiled=True)  4.24 us
  transfers between devices with their start and end apart: 2, of which 2 were waited for; matrix products, arithmetic and copies ran while one was open for 4% of the time, Pallas kernels for 0%

profile of v1, /device:TPU:0, one launch (start us, length us, event | category | flops | bytes accessed | tf_op | source)
XLA Modules:
  0.0 174.6 jit_solution(7806024913928752817)
XLA Ops:
  7.2 0.0 copy-start
  7.2 0.0 all-gather.4.cloned.1.call-start
  7.2 5.1 %cash_rows.1 = bf16[128,512]{1,0:T(8,128)(2,1)} custom-call(s32[1]{0:T(128)} %bitcast.3.base_ref, s32[16,2048]{1,0:T(8,128)} %bitcast.32, f32[16,2048]{1,0:T(8,128)} %bitcast.33, s32[1,2048]{1,0:T(1,128)} %set_ref.1), custom_call_target="tpu_custom_call" | custom-call | flops 536870912 | bytes 131072 | tf_op jit(solution)/shard_map/cash_rows/pallas_call | solution.py:60
  12.3 0.0 all-gather.4.cloned.1.call-update
  12.3 2.4 %copy.12 = bf16[1,2,64,2048]{2,1,0,3:T(2,128)(2,1)S(1)} copy(bf16[1,2,64,2048]{3,2,1,0:T(8,128)(2,1)} %param.6) | data formatting | bytes 1048576 | tf_op args[0]
  14.7 1.5 reshape.54
  16.2 4.2 %all-to-all-start = ((bf16[4,2,32768]{2,1,0:T(2,128)(2,1)}), bf16[4,2,32768]{2,1,0:T(2,128)(2,1)S(1)}, u32[]{:S(2)}, u32[]{:S(2)}) async-start(bf16[4,2,32768]{2,1,0:T(2,128)(2,1)} %reshape.54), calls=%async_computation | async-start | bytes 1048576 | tf_op jit(solution)/shard_map/all_to_all | solution.py:167
  20.5 0.0 copy-done
  20.5 0.8 fusion.date_ref
  21.2 0.1 iota_compare_fusion
  21.3 8.9 %all-to-all-done = bf16[4,2,32768]{2,1,0:T(2,128)(2,1)S(1)} async-done(((bf16[4,2,32768]{2,1,0:T(2,128)(2,1)}), bf16[4,2,32768]{2,1,0:T(2,128)(2,1)S(1)}, u32[]{:S(2)}, u32[]{:S(2)}) %all-to-all-start) | async-done | bytes 524320 | tf_op jit(solution)/shard_map/all_to_all | solution.py:167
  30.2 0.7 reshape.55
  30.9 1.8 %copy.14 = bf16[1,2,64,4,512]{4,2,1,3,0:T(8,128)(2,1)} copy(bf16[1,2,64,4,512]{2,1,4,3,0:T(2,128)(2,1)S(1)} %bitcast.25) | data formatting | bytes 1048576 | tf_op jit(solution)/shard_map/all_to_all | solution.py:167
  32.8 44.6 %all-gather.4.cloned.1.call-done.cash_ref = bf16[4096,512]{1,0:T(8,128)(2,1)} async-done(((bf16[128,512]{1,0:T(8,128)(2,1)}), bf16[4096,512]{1,0:T(8,128)(2,1)}) %all-gather.4.cloned.1.call-update) | async-done | bytes 4194320 | tf_op jit(solution)/shard_map/all_gather | solution.py:169
  77.4 20.2 %price_dates.1 = (f32[2,1,512]{2,1,0:T(1,128)}, f32[2,4,64]{2,1,0:T(4,128)}) custom-call(s32[2]{0:T(128)} %fusion.date_ref, bf16[4,2,64,512]{3,2,1,0:T(8,128)(2,1)} %bitcast.27, bf16[4096,512]{1,0:T(8,128)(2,1)} %all-gather.4.cloned.1.call-done.cash_ref, f32[16,512]{1,0:T(8,128)} %dw_ref.1), custom_call_target="tpu_custom_call" | custom-call | flops 9126805504 | bytes 4194304 | tf_op jit(solution)/shard_map/price_dates/pallas_call | solution.py:133
  97.6 0.8 reshape.45
  98.3 0.7 copy.19
  99.0 67.2 %all-gather.1 = f32[32,2,768]{2,1,0:T(2,128)S(1)} all-gather(f32[1,2,768]{2,1,0:T(2,128)S(1)} %maximum_bitcast_fusion), channel_id=2, replica_groups=mesh['ccy'=4,'path'=8] {'ccy','path'}, dimensions={0}, use_global_device_ids=true | all-gather | bytes 202752 | tf_op jit(solution)/shard_map/all_gather | solution.py:175
  166.2 0.1 constant_dynamic-slice_fusion.1
  166.4 0.7 select_reduce_fusion.1
  167.1 0.7 select_reduce_fusion
  (5 shorter events, 0.0 us)
Async XLA Ops:
  7.2 13.3 %copy-start = (s32[16]{0:T(128)S(1)}, s32[16]{0:T(128)}, u32[]{:S(2)}) copy-start(s32[16]{0:T(128)} %param.10) | copy-start | bytes 196
  7.2 70.2 %all-gather.4.cloned.1.call-start = ((), (), s32[]{:S(2)}) async-start(), calls=%async_computation.1 | async-start | bytes 4325376 | tf_op jit(solution)/shard_map/all_gather | solution.py:169
  16.2 14.0 %all-to-all-start = ((bf16[4,2,32768]{2,1,0:T(2,128)(2,1)}), bf16[4,2,32768]{2,1,0:T(2,128)(2,1)S(1)}, u32[]{:S(2)}, u32[]{:S(2)}) async-start(bf16[4,2,32768]{2,1,0:T(2,128)(2,1)} %reshape.54), calls=%async_computation | async-start | bytes 1048576 | tf_op jit(solution)/shard_map/all_to_all | solution.py:167
Sparse Core Ops, SparseCore 0:
  12.4 64.9 all-gather.3

commit v2 on v1

--- a/solution.py
+++ b/solution.py
@@ -155,34 +155,210 @@
     )(dates, curves, cash, default_weight)
 
 
+def exchange_kernel(chunk_ref, curve_ref, cash_ref, curves_ref, send, recv, own):
+    groups, members = cash_ref.shape[0], cash_ref.shape[1]
+    share = curves_ref.shape[3]
+    c, p = lax.axis_index("ccy"), lax.axis_index("path")
+    levels = members // 2
+    z, y = p // 2, p % 2
+    sibling = c + 1 - 2 * (c % 2)
+    across = (c + 2) % groups
+    beside = p + 1 - 2 * y
+    peers = [((c + d) % groups, p) for d in range(1, groups)] + [(c, beside)]
+    peers += [(c, ((z + k) % levels) * 2 + y) for k in range(1, levels)]
+    barrier = pltpu.get_barrier_semaphore()
+    for peer in peers:
+        pl.semaphore_signal(barrier, inc=1, device_id=peer, device_id_type=pl.DeviceIdType.MESH)
+    pl.semaphore_wait(barrier, len(peers))
+
+    started = []
+
+    def remote(src, dst, device):
+        k = len(started)
+        copy = pltpu.make_async_remote_copy(
+            src_ref=src, dst_ref=dst, send_sem=send.at[k], recv_sem=recv.at[k],
+            device_id=device, device_id_type=pl.DeviceIdType.MESH,
+        )
+        copy.start()
+        started.append(copy)
+        return copy
+
+    near, far, core = (c, beside), (across, p), (sibling, p)
+    mine = cash_ref.at[c, p]
+    up = []
+    for k in range(1, levels):
+        up.append((k, remote(chunk_ref, mine, (c, ((z + k) % levels) * 2 + y))))
+    late = []
+    for d in range(1, groups):
+        t = (c + d) % groups
+        cols = pl.ds(pl.multiple_of(t * share, 128), share)
+        late.append(remote(curve_ref.at[:, :, cols], curves_ref.at[c], (t, p)))
+    keep = [
+        pltpu.make_async_copy(chunk_ref, mine, own.at[0]),
+        pltpu.make_async_copy(
+            curve_ref.at[:, :, pl.ds(pl.multiple_of(c * share, 128), share)], curves_ref.at[c], own.at[1]
+        ),
+    ]
+    for copy in keep:
+        copy.start()
+
+    second = []
+
+    def spread(source, q):
+        other = q + 1 - 2 * y
+        a = remote(source.at[0], cash_ref.at[c, q, 0], near)
+        b = remote(source.at[1], cash_ref.at[c, q, 1], far)
+        second.append((a, b, q, other))
+        late.append(remote(source.at[0], cash_ref.at[c, q, 0], far))
+        late.append(remote(source.at[1], cash_ref.at[c, q, 1], near))
+        late.append(remote(source, cash_ref.at[c, q], core))
+
+    third = []
+    spread(chunk_ref, p)
+    for k, copy in up:
+        copy.wait_recv()
+        q = ((z - k + levels) % levels) * 2 + y
+        spread(cash_ref.at[c, q], q)
+    for a, b, q, other in second:
+        a.wait_recv()
+        block = cash_ref.at[c, other, 0]
+        third.append((remote(block, block, far), cash_ref.at[across, other, 0]))
+        late.append(remote(block, block, core))
+        b.wait_recv()
+        block = cash_ref.at[across, q, 1]
+        third.append((remote(block, block, near), cash_ref.at[across, other, 1]))
+        late.append(remote(block, block, core))
+    first = 0
+    for a, b, q, other in second:
+        base = len(up) + groups - 1 + 5 * first
+        first += 1
+        started[base + 2].wait_recv()
+        block = cash_ref.at[across, q, 0]
+        late.append(remote(block, block, core))
+        started[base + 3].wait_recv()
+        block = cash_ref.at[c, other, 1]
+        late.append(remote(block, block, core))
+    for copy, block in third:
+        copy.wait_recv()
+        late.append(remote(block, block, core))
+    passed = {id(started[len(up) + groups - 1 + 5 * n + m]) for n in range(levels) for m in (2, 3)}
+    for copy in late:
+        if id(copy) not in passed:
+            copy.wait_recv()
+    for copy in started:
+        copy.wait_send()
+    for copy in keep:
+        copy.wait()
+
+
+def exchange(chunk, curve_store, groups, members):
+    rows, nsets = chunk.shape
+    _, slots, nodes, paths = curve_store.shape
+    levels = members // 2
+    count = levels - 1 + groups - 1 + 5 * levels + 4 * levels + 2 * levels + 2 * levels
+    hbm = pl.BlockSpec(memory_space=pl.ANY)
+    vmem = pl.BlockSpec(memory_space=pltpu.VMEM)
+    cash, curves = pl.pallas_call(
+        exchange_kernel,
+        out_shape=[
+            jax.ShapeDtypeStruct((groups, members, 2, rows // 2, nsets), chunk.dtype),
+            jax.ShapeDtypeStruct((groups, slots, nodes, paths // groups), curve_store.dtype),
+        ],
+        in_specs=[vmem, vmem],
+        out_specs=[hbm, hbm],
+        scratch_shapes=[
+            pltpu.SemaphoreType.DMA((count,)),
+            pltpu.SemaphoreType.DMA((count,)),
+            pltpu.SemaphoreType.DMA((2,)),
+        ],
+        compiler_params=pltpu.CompilerParams(collective_id=0, has_side_effects=True),
+        name="exchange",
+    )(chunk.reshape(2, rows // 2, nsets), curve_store[0])
+    return cash.reshape(groups * members * rows, nsets), curves
+
+
+def collect_kernel(groups, members, part_ref, out_ref, held, send, recv, own):
+    c, p = lax.axis_index("ccy"), lax.axis_index("path")
+    steps = [(dc, dp) for dc in range(groups) for dp in range(members)][1:]
+    barrier = pltpu.get_barrier_semaphore()
+    targets = [((c + dc) % groups, (p + dp) % members) for dc, dp in steps]
+    for target in targets:
+        pl.semaphore_signal(barrier, inc=1, device_id=target, device_id_type=pl.DeviceIdType.MESH)
+    keep = pltpu.make_async_copy(part_ref.at[c], held.at[c, p], own.at[0])
+    keep.start()
+    pl.semaphore_wait(barrier, len(targets))
+    copies = []
+    for k, target in enumerate(targets):
+        copy = pltpu.make_async_remote_copy(
+            src_ref=part_ref.at[target[0]], dst_ref=held.at[c, p], send_sem=send.at[k],
+            recv_sem=recv.at[k], device_id=target, device_id_type=pl.DeviceIdType.MESH,
+        )
+        copy.start()
+        copies.append(copy)
+    keep.wait()
+    for copy in copies:
+        copy.wait()
+    total = held[0]
+    for g in range(1, groups):
+        total = total + held[g]
+    out_ref[...] = total
+
+
+def collect(part, members):
+    groups = part.shape[0]
+    links = groups * members - 1
+    vmem = pl.BlockSpec(memory_space=pltpu.VMEM)
+    return pl.pallas_call(
+        functools.partial(collect_kernel, groups, members),
+        out_shape=jax.ShapeDtypeStruct((members,) + part.shape[1:], jnp.float32),
+        in_specs=[vmem],
+        out_specs=vmem,
+        scratch_shapes=[
+            pltpu.VMEM((groups, members) + part.shape[1:], jnp.float32),
+            pltpu.SemaphoreType.DMA((links,)),
+            pltpu.SemaphoreType.DMA((links,)),
+            pltpu.SemaphoreType.DMA((1,)),
+        ],
+        compiler_params=pltpu.CompilerParams(collective_id=1, has_side_effects=True),
+        name="collect",
+    )(part)
+
+
 def by_slot(curve_store, cash_index, cash_amount, trade_set, date_slot, default_weight):
     groups, members = lax.axis_size("ccy"), lax.axis_size("path")
-    group_index, path_index = lax.axis_index("ccy"), lax.axis_index("path")
+    path_index = lax.axis_index("path")
     slots = curve_store.shape[1]
     nodes = curve_store.shape[2]
     total_paths = curve_store.shape[3]
     rows = CFG // members
     nsets = default_weight.shape[1]
     base = (path_index * rows).astype(jnp.int32)[None]
-    curves = lax.all_to_all(curve_store, "ccy", split_axis=3, concat_axis=0, tiled=True)
     chunk = build_cash(base, cash_index[0], cash_amount[0], trade_set[0], rows, nsets)
-    cash = lax.all_gather(chunk, ("ccy", "path"), axis=0, tiled=True)
+    if groups == 4 and members % 2 == 0:
+        cash, curves = exchange(chunk, curve_store, groups, members)
+    else:
+        curves = lax.all_to_all(curve_store, "ccy", split_axis=3, concat_axis=0, tiled=True)
+        cash = lax.all_gather(chunk, ("ccy", "path"), axis=0, tiled=True)
     own = path_index * slots + jnp.arange(slots, dtype=jnp.int32)
     numbers = jnp.arange(date_slot.shape[0], dtype=jnp.int32)
     dates = jnp.sum(jnp.where(date_slot[None, :] == own[:, None], numbers[None, :], 0), axis=1).astype(jnp.int32)
     exposure_part, sens_part = run_main(dates, curves, cash, default_weight, total_paths)
-    part = jnp.concatenate([exposure_part[:, 0, :], sens_part.reshape(slots, groups * nodes)], axis=1)
-    parts = lax.all_gather(part, ("ccy", "path"), axis=0)
     share = nsets // groups
-    exposure = lax.dynamic_slice_in_dim(parts, group_index * share, share, 2)
-    sens = lax.dynamic_slice_in_dim(parts, nsets + group_index * nodes, nodes, 2)
+    exposure_part = jnp.transpose(exposure_part.reshape(slots, groups, share), (1, 0, 2))
+    sens_part = jnp.transpose(sens_part, (1, 0, 2))
+    sens_part = jnp.pad(sens_part, ((0, 0), (0, 0), (0, max(share - nodes, 0))))
+    exposure_part = jnp.pad(exposure_part, ((0, 0), (0, 0), (0, max(nodes - share, 0))))
+    part = jnp.concatenate([exposure_part, sens_part], axis=1)
+    part = jnp.pad(part, ((0, 0), (0, -2 * slots % 8), (0, 0)))
+    sums = collect(part, members)
+    hit = date_slot[:, None, None] == jnp.arange(members * slots, dtype=jnp.int32)[None, :, None]
 
     def finish(block):
-        rows_by_slot = jnp.sum(block.reshape(groups, members * slots, -1), axis=0)
-        hit = date_slot[:, None, None] == jnp.arange(members * slots, dtype=jnp.int32)[None, :, None]
-        return jnp.sum(jnp.where(hit, rows_by_slot[None], 0.0), axis=1)
-
-    return (finish(exposure), finish(sens)[None])
+        return jnp.sum(jnp.where(hit, block.reshape(1, members * slots, -1), 0.0), axis=1)
+
+    exposure = finish(sums[:, :slots, :share])
+    sens = finish(sums[:, slots : 2 * slots, :nodes])
+    return (exposure, sens[None])
 
 
 def by_path(curve_store, cash_index, cash_amount, trade_set, date_slot, default_weight):

time: 175 us -> 76.7 us (0.44)
  blocking collectives: 67.2 us -> 0 us
  waiting for transfers between devices: 53.6 us -> 0 us
  Pallas kernels: 25.2 us -> 69.2 us
  between operations: 14.1 us -> 0.67 us
  local copies, waits for them, and re-layouts: 8.02 us -> 3.51 us
  starting transfers between devices: 4.27 us -> 0 us
    all_gather x1 -> x0, blocking collectives: 67.2 us -> none  [by_slot(): parts = lax.all_gather(part, ('ccy', 'path'), axis=0)]
    all_gather x1 -> x0, waiting for transfers between devices: 44.6 us -> none  [by_slot(): cash = lax.all_gather(chunk, ('ccy', 'path'), axis=0, tiled=True)]
    pallas_call x0 -> x2, Pallas kernels: none -> 44 us  [the longest x1 33.1 us: exchange(): pl.pallas_call(exchange_kernel, out_shape=[jax.ShapeDtypeStruct((groups,...]
    all_to_all x1 -> x0, waiting for transfers between devices: 8.91 us -> none  [by_slot(): lax.all_to_all(curve_store, 'ccy', split_axis=3, concat_axis=0, tiled=True)]
    unnamed x6 -> x2, local copies, waits for them, and re-layouts: 5.31 us -> 0.01 us
    all_to_all x1 -> x0, starting transfers between devices: 4.24 us -> none  [by_slot(): lax.all_to_all(curve_store, 'ccy', split_axis=3, concat_axis=0, tiled=True)]
    all_to_all x1 -> x0, local copies, waits for them, and re-layouts: 1.84 us -> none  [by_slot(): lax.all_to_all(curve_store, 'ccy', split_axis=3, concat_axis=0, tiled=True)]
  transfers between devices with their start and end apart: 2 -> 0, of which waited for: 2 -> 0; matrix products, arithmetic and copies ran while one was open for 4% -> 0% of each run, Pallas kernels for 0% -> 0%
where the time goes in v2:
time: 76.7 us; the launch traced here: 76.2 us
  Pallas kernels  69.2 us (90%)
  local copies, waits for them, and re-layouts  3.51 us (5%)
  other arithmetic  2.84 us (4%)
    pallas_call x1, Pallas kernels, exchange(): pl.pallas_call(exchange_kernel, out_shape=[jax.ShapeDtypeStruct((groups,...  33.1 us
    pallas_call x1, Pallas kernels, run_main(): pl.pallas_call(functools.partial(main_kernel, groups, cfg, total_paths),...  20.2 us
    pallas_call x1, Pallas kernels, collect(): pl.pallas_call(functools.partial(collect_kernel, groups, members), out_sh...  11 us
    pallas_call x1, Pallas kernels, build_cash(): pl.pallas_call(functools.partial(cash_kernel, rows), out_shape=jax.ShapeD...  5.06 us

profile of v2, /device:TPU:0, one launch (start us, length us, event | category | flops | bytes accessed | tf_op | source)
XLA Modules:
  0.0 76.2 jit_solution(7922988674632227782)
XLA Ops:
  0.6 5.1 %cash_rows.1 = bf16[128,512]{1,0:T(8,128)(2,1)} custom-call(s32[1]{0:T(128)} %bitcast.base_ref, s32[16,2048]{1,0:T(8,128)} %bitcast.29, f32[16,2048]{1,0:T(8,128)} %bitcast.30, s32[1,2048]{1,0:T(1,128)} %set_ref.1), custom_call_target="tpu_custom_call" | custom-call | flops 536870912 | bytes 131072 | tf_op jit(solution)/shard_map/cash_rows/pallas_call | solution.py:60
  5.7 33.1 %exchange.1 = (bf16[4,8,2,64,512]{4,3,2,1,0:T(8,128)(2,1)}, bf16[4,2,64,512]{3,2,1,0:T(8,128)(2,1)}) custom-call(bf16[2,64,512]{2,1,0:T(8,128)(2,1)} %bitcast.21, bf16[2,64,2048]{2,1,0:T(8,128)(2,1)} %bitcast.20), custom_call_target="tpu_custom_call" | custom-call | tf_op jit(solution)/shard_map/exchange/pallas_call | solution.py:261
  38.8 1.3 %fusion.date_ref = s32[2]{0:T(128)} fusion(s32[16]{0:T(128)} %param.10, s32[2]{0:T(128)S(1)} %iota_add_fusion), kind=kLoop, calls=%fused_computation.8 | loop fusion | flops 94 | bytes 80 | tf_op jit(solution)/shard_map/reduce_sum | solution.py:344
  40.1 0.0 copy-start
  40.1 20.2 %price_dates.1 = (f32[2,1,512]{2,1,0:T(1,128)}, f32[2,4,64]{2,1,0:T(4,128)}) custom-call(s32[2]{0:T(128)} %fusion.date_ref, bf16[4,2,64,512]{3,2,1,0:T(8,128)(2,1)} %get-tuple-element.6.curve_ref, bf16[4096,512]{1,0:T(8,128)(2,1)} %bitcast.28, f32[16,512]{1,0:T(8,128)} %dw_ref.1), custom_call_target="tpu_custom_call" | custom-call | flops 9126805504 | bytes 4194304 | tf_op jit(solution)/shard_map/price_dates/pallas_call | solution.py:133
  60.3 0.7 copy.15
  60.9 0.7 copy.16
  61.6 0.6 pad.9.part_ref
  62.2 11.0 %collect.1 = f32[8,8,128]{2,1,0:T(8,128)} custom-call(f32[4,8,128]{2,1,0:T(8,128)} %pad.9.part_ref), custom_call_target="tpu_custom_call" | custom-call | tf_op jit(solution)/shard_map/collect/pallas_call | solution.py:311
  73.2 0.8 %slice.7 = f32[8,2,64]{2,1,0:T(2,128)S(1)} slice(f32[8,8,128]{2,1,0:T(8,128)} %collect.1), slice={[0:8], [2:4], [0:64]} | slice | bytes 8192 | tf_op jit(solution)/shard_map/slice | solution.py:360
  74.0 0.0 copy-done
  74.0 0.1 iota_compare_fusion.1
  74.1 0.7 select_reduce_fusion
  74.8 0.8 slice.6
  75.5 0.7 select_reduce_fusion.1
  (2 shorter events, 0.0 us)
Async XLA Ops:
  40.1 33.9 %copy-start = (s32[16]{0:T(128)S(1)}, s32[16]{0:T(128)}, u32[]{:S(2)}) copy-start(s32[16]{0:T(128)} %param.10) | copy-start | bytes 196
